TPU v7x, 128 devices: a whole 4x4x4 slice. The times are simulated.
128 devices in a mesh: mx: 4 (over z), my: 4 (over y_hi, core), col: 8 (over y_lo, x).
Axes of the slice: x: 4, y: 4 (y_hi: 2, y_lo: 2; y = y_hi * 2 + y_lo), z: 4, core: 2. Of those that a mesh axis runs over, the one named last changes fastest.
Arguments:
- spectrum: float32 [2, 16, 128, 32, 512], P(None, 'col', None, 'mx', 'my'), may hold values from -6 to 6
- core_tensor: float32 [2, 64, 64, 16, 16, 16], P(None, 'col', None, ('mx', 'my')), may hold values from -0.01171875 to 0.01171875
- input_factor: float32 [128, 64], replicated, may hold values from -0.5 to 0.5
- output_factor: float32 [128, 64], replicated, may hold values from -0.75 to 0.75
- first_factor: float32 [32, 16], P('mx'), may hold values from -5 to 5
- second_factor: float32 [32, 16], P('my'), may hold values from -5 to 5
- third_factor: float32 [16, 16], replicated, may hold values from -5 to 5
Outputs:
- mixed_modes: float32 [2, 16, 128, 32, 512], P(None, 'col', None, 'mx', 'my')
All inputs are finite; a program needn't handle non-finite values.
Results may differ from a plain program's by a relative error of at most 0.00007.
Values sent between devices are 32-bit elements; how exact they have to be, the bound alone decides.
No kernel may reach another device: no remote copies, remote signals or barrier semaphores. Data moves between devices by JAX's collectives and lax.ppermute only.
A program may use at most 128 MiB of HBM per device.

v0:
```python
import jax
import jax.numpy as jnp
from jax import lax
from jax.sharding import PartitionSpec as P

precise = lax.Precision.HIGHEST


def per_device(
    spectrum, core_tensor, input_factor, output_factor, first_factor, second_factor, third_factor
):
    rank_local = core_tensor.shape[1]
    rank_out = core_tensor.shape[2]
    rows_first = first_factor.shape[0]
    rank_second = second_factor.shape[1]
    modes_third = third_factor.shape[0]
    core_third = jnp.einsum("cpqstu,zu->cpqstz", core_tensor, third_factor, precision=precise)
    core_third = core_third.reshape(
        2, rank_local, rank_out, core_tensor.shape[3], rank_second * modes_third
    )
    core_gathered = lax.all_gather(core_third, ("mx", "my"), axis=3, tiled=True)
    weight_first = jnp.einsum("cpqsm,ks->cpqkm", core_gathered, first_factor, precision=precise)
    weight_first = weight_first.reshape(
        2, rank_local, rank_out, rows_first, rank_second, modes_third
    )
    mode_weight = jnp.einsum("cpqktz,yt->cpqkyz", weight_first, second_factor, precision=precise)
    mode_weight = mode_weight.reshape(2, rank_local, rank_out, rows_first, -1)
    projected = jnp.einsum("cbikm,ir->cbrkm", spectrum, input_factor, precision=precise)
    rank_spectrum = lax.all_to_all(projected, "col", split_axis=2, concat_axis=1, tiled=True)
    real_part = jnp.einsum(
        "brkm,rqkm->bqkm", rank_spectrum[0], mode_weight[0], precision=precise
    ) - jnp.einsum("brkm,rqkm->bqkm", rank_spectrum[1], mode_weight[1], precision=precise)
    imag_part = jnp.einsum(
        "brkm,rqkm->bqkm", rank_spectrum[0], mode_weight[1], precision=precise
    ) + jnp.einsum("brkm,rqkm->bqkm", rank_spectrum[1], mode_weight[0], precision=precise)
    mode_values = jnp.stack([real_part, imag_part])
    summed_values = lax.psum_scatter(mode_values, "col", scatter_dimension=1, tiled=True)
    mixed_modes = jnp.einsum("oq,cbqkm->cbokm", output_factor, summed_values, precision=precise)
    return mixed_modes


def solution(mesh):
    placed = (
        P(None, "col", None, "mx", "my"),
        P(None, "col", None, ("mx", "my"), None, None),
        P(),
        P(),
        P("mx", None),
        P("my", None),
        P(),
    )
    return jax.shard_map(
        per_device,
        mesh=mesh,
        in_specs=placed,
        out_specs=P(None, "col", None, "mx", "my"),
        check_vma=False,
    )
```

profile of v0, /device:TPU:1, one launch (start us, length us, event | category | flops | bytes accessed | tf_op | source)
XLA Modules:
  0.0 377.2 jit_solution(9555578541024835973)
XLA Ops:
  6.5 0.0 copy-start
  6.5 0.0 copy-start.4
  6.5 0.0 all-gather.2.cloned.1.call-start
  6.5 1.6 copy-done
  8.1 3.9 %fusion.22 = f32[2,8,64,16,16]{2,4,3,1,0:T(8,128)} fusion(f32[2,8,64,1,16,16]{2,5,4,3,1,0:T(8,128)S(1)} %copy-done, f32[16,16]{1,0:T(8,128)} %param.13), kind=kOutput, calls=%fused_computation.17 | convolution fusion | flops 50331648 | bytes 2098176 | tf_op jit(solution)/shard_map/cpqstu,zu->cpqstz/dot_general | solution.py:17
  12.1 3.2 copy.51
  15.2 0.0 all-gather.2.cloned.1.call-update
  15.2 0.0 reduce-scatter.2.cloned.1.call-start
  15.3 0.0 copy-done.4
  15.3 3.1 fusion.26
  18.4 0.6 copy.57
  19.0 20.6 %all_to_all.15 = f32[2,2,64,8,128]{4,3,1,0,2:T(8,128)S(1)} all-to-all(f32[2,2,64,8,128]{4,3,1,0,2:T(8,128)S(1)} %copy.57), channel_id=1, replica_groups=mesh['mx'=4,'my'=4,'col'=8] {'col'}, dimensions={2} | all-to-all | bytes 2097152 | tf_op jit(solution)/shard_map/all_to_all | solution.py:29
  39.6 0.1 copy.58
  39.7 0.1 fusion.36
  39.9 0.0 copy-start.6
  39.9 3.2 copy.61
  43.1 3.1 copy.65
  46.2 90.1 %all-gather.2.cloned.1.call-done = f32[2,8,64,16,256]{4,2,1,0,3:T(8,128)} async-done(((f32[2,8,64,1,256]{4,2,1,0,3:T(8,128)}), f32[2,8,64,16,256]{4,2,1,0,3:T(8,128)}) %all-gather.2.cloned.1.call-update) | async-done | bytes 16777232 | tf_op jit(solution)/shard_map/all_gather | solution.py:21
  136.3 0.0 copy-done.6
  136.3 25.8 %fusion.16 = f32[2,8,64,8,256]{4,3,2,1,0:T(8,128)} fusion(f32[2,8,64,16,256]{4,2,1,0,3:T(8,128)} %all-gather.2.cloned.1.call-done, f32[8,16]{1,0:T(8,128)S(1)} %copy-done.6), kind=kOutput, calls=%fused_computation.15 | convolution fusion | flops 402653184 | bytes 25166336 | tf_op jit(solution)/shard_map/cpqsm,ks->cpqkm/dot_general | solution.py:22
  162.1 0.0 copy-start.7
  162.1 12.2 %copy.53 = f32[2,8,64,8,256]{2,4,3,1,0:T(8,128)} copy(f32[2,8,64,8,256]{4,3,2,1,0:T(8,128)} %fusion.16) | data formatting | bytes 16777216 | tf_op jit(solution)/shard_map/cpqsm,ks->cpqkm/transpose | solution.py:22
  174.3 0.0 copy-done.7
  174.4 17.9 %fusion.19 = f32[2,8,64,8,8,16]{2,4,5,3,1,0:T(8,128)S(1)} fusion(f32[2,8,64,8,16,16]{2,5,4,3,1,0:T(8,128)} %bitcast.59, f32[8,16]{1,0:T(8,128)S(1)} %copy-done.7), kind=kOutput, calls=%fused_computation.16 | convolution fusion | flops 201326592 | bytes 12583424 | tf_op jit(solution)/shard_map/cpqktz,yt->cpqkyz/dot_general | solution.py:26
  192.2 1.1 fusion.35
  193.3 0.9 copy.55
  194.2 0.0 copy-start.2
  194.2 0.9 copy.62
  195.2 1.2 copy-done.2
  196.4 0.0 copy-start.3
  196.4 14.4 %fusion.4 = f32[8,128,64,16]{2,3,1,0:T(8,128)S(1)} fusion(f32[16,8,8,128]{0,1,3,2:T(8,128)S(1)} %copy-done.2, f32[8,64,8,128]{1,3,2,0:T(8,128)S(1)} %bitcast.60), kind=kOutput, calls=%fused_computation.7 | convolution fusion | flops 100663296 | bytes 6815744 | tf_op jit(solution)/shard_map/brkm,rqkm->bqkm/dot_general | solution.py:33
  210.8 0.0 copy-done.3
  210.8 14.6 %fusion.6 = f32[8,128,64,16]{2,3,1,0:T(8,128)S(1)} fusion(f32[16,8,8,128]{0,1,3,2:T(8,128)S(1)} %copy-done.3, f32[8,64,8,128]{1,3,2,0:T(8,128)S(1)} %bitcast.61), kind=kOutput, calls=%fused_computation.9 | convolution fusion | flops 100663296 | bytes 6815744 | tf_op jit(solution)/shard_map/brkm,rqkm->bqkm/dot_general | solution.py:32
  225.4 14.3 %add_bitcast_fusion = f32[1,16,64,8,128]{2,1,4,3,0:T(8,128)S(1)} fusion(f32[8,128,64,16]{2,3,1,0:T(8,128)S(1)} %fusion.4, f32[16,8,8,128]{0,1,3,2:T(8,128)S(1)} %copy-done.3, f32[8,64,8,128]{1,3,2,0:T(8,128)S(1)} %bitcast.57), kind=kOutput, calls=%fused_computation.5 | convolution fusion | flops 101711872 | bytes 11010048 | tf_op jit(solution)/shard_map/brkm,rqkm->bqkm/dot_general | solution.py:35
  239.8 14.4 %subtract_bitcast_fusion = f32[1,16,64,8,128]{2,1,4,3,0:T(8,128)S(1)} fusion(f32[8,128,64,16]{2,3,1,0:T(8,128)S(1)} %fusion.6, f32[16,8,8,128]{0,1,3,2:T(8,128)S(1)} %copy-done.2, f32[8,64,8,128]{1,3,2,0:T(8,128)S(1)} %bitcast.58), kind=kOutput, calls=%fused_computation.6 | convolution fusion | flops 101711872 | bytes 11010048 | tf_op jit(solution)/shard_map/brkm,rqkm->bqkm/dot_general | solution.py:30
  254.2 6.1 %pad_maximum_fusion = f32[2,16,64,8,128]{2,1,4,3,0:T(8,128)} fusion(f32[1,16,64,8,128]{2,1,4,3,0:T(8,128)S(1)} %add_bitcast_fusion, f32[1,16,64,8,128]{2,1,4,3,0:T(8,128)S(1)} %subtract_bitcast_fusion), kind=kLoop, calls=%fused_computation | loop fusion | flops 2097152 | bytes 16777216 | tf_op jit(solution)/shard_map/stack | solution.py:36
  260.3 11.0 %copy.70 = f32[2,16,64,8,128]{4,3,2,0,1:T(8,128)} copy(f32[2,16,64,8,128]{2,1,4,3,0:T(8,128)} %pad_maximum_fusion) | data formatting | bytes 16777216 | tf_op jit(solution)/shard_map/stack | solution.py:36
  271.3 0.0 copy-start.5
  271.3 0.0 reduce-scatter.2.cloned.1.call-update
  271.3 0.0 copy-start.1
  271.3 89.9 %reduce-scatter.2.cloned.1.call-done = f32[2,2,64,8,128]{4,3,2,0,1:T(8,128)} async-done(((f32[2,16,64,8,128]{4,3,2,0,1:T(8,128)}), f32[2,2,64,8,128]{4,3,2,0,1:T(8,128)}) %reduce-scatter.2.cloned.1.call-update) | async-done | bytes 1048592 | tf_op jit(solution)/shard_map/reduce_scatter | solution.py:37
  361.2 0.0 copy-done.5
  361.2 6.0 %convolution_bitcast_fusion = f32[2,2,128,8,128]{2,4,3,1,0:T(8,128)} fusion(f32[2,2,64,8,128]{4,3,2,0,1:T(8,128)} %reduce-scatter.2.cloned.1.call-done, f32[128,64]{0,1:T(8,128)S(1)} %copy-done.5), kind=kOutput, calls=%fused_computation.21 | convolution fusion | flops 402653184 | bytes 3178496 | tf_op jit(solution)/shard_map/oq,cbqkm->cbokm/dot_general | solution.py:38
  367.2 2.9 copy.72
  370.1 0.0 copy-done.1
  (2 shorter events, 0.1 us)
Async XLA Ops:
  6.5 1.6 copy-start
  6.5 8.8 %copy-start.4 = (f32[128,64]{0,1:T(8,128)S(1)}, f32[128,64]{0,1:T(8,128)}, u32[]{:S(2)}) copy-start(f32[128,64]{0,1:T(8,128)} %param.9) | copy-start | bytes 98308
  6.5 129.7 %all-gather.2.cloned.1.call-start = ((), (), s32[]{:S(2)}) async-start(), calls=%async_computation.2 | async-start | bytes 17825792 | tf_op jit(solution)/shard_map/all_gather | solution.py:21
  15.2 346.0 %reduce-scatter.2.cloned.1.call-start = ((), (), s32[]{:S(2)}) async-start(), calls=%async_computation.3 | async-start | bytes 9437184 | tf_op jit(solution)/shard_map/reduce_scatter | solution.py:37
  39.9 96.3 %copy-start.6 = (f32[8,16]{1,0:T(8,128)S(1)}, f32[8,16]{1,0:T(8,128)}, u32[]{:S(2)}) copy-start(f32[8,16]{1,0:T(8,128)} %param.11) | copy-start | bytes 1540
  162.1 12.2 %copy-start.7 = (f32[8,16]{1,0:T(8,128)S(1)}, f32[8,16]{1,0:T(8,128)}, u32[]{:S(2)}) copy-start(f32[8,16]{1,0:T(8,128)} %param.12) | copy-start | bytes 1540
  194.2 2.2 copy-start.2
  196.4 14.4 %copy-start.3 = (f32[16,8,8,128]{0,1,3,2:T(8,128)S(1)}, f32[16,8,8,128]{0,1,3,2:T(8,128)}, u32[]{:S(2)}) copy-start(f32[16,8,8,128]{0,1,3,2:T(8,128)} %copy.65) | copy-start | bytes 1572868
  271.3 89.9 %copy-start.5 = (f32[128,64]{0,1:T(8,128)S(1)}, f32[128,64]{0,1:T(8,128)}, u32[]{:S(2)}) copy-start(f32[128,64]{0,1:T(8,128)} %param.10) | copy-start | bytes 98308
  271.3 98.8 %copy-start.1 = (f32[2,8,64,1,16,16]{2,5,4,3,1,0:T(8,128)S(1)}, f32[2,8,64,1,16,16]{2,5,4,3,1,0:T(8,128)}, u32[]{:S(2)}) copy-start(f32[2,8,64,1,16,16]{2,5,4,3,1,0:T(8,128)} %param.8) | copy-start | bytes 3145732
Sparse Core Ops, SparseCore 0:
  15.4 120.8 all-gather.1
  271.4 89.7 reduce-scatter.1
where the time goes:
time: 383 us; the launch traced here: 377 us
  waiting for transfers between devices  180 us (47%)
  matrix products  114 us (30%)
  local copies, waits for them, and re-layouts  42.2 us (11%)
  blocking collectives  20.6 us (5%)
  between operations  13.8 us (4%)
  other arithmetic  6.1 us (2%)
    all_gather x1, waiting for transfers between devices, per_device(): core_gathered = lax.all_gather(core_third, ('mx', 'my'), axis=3, tiled=True)  90.1 us
    reduce_scatter x1, waiting for transfers between devices, per_device(): lax.psum_scatter(mode_values, 'col', scatter_dimension=1, tiled=True)  89.9 us
    dot_general x1, matrix products, per_device(): jnp.einsum('cpqsm,ks->cpqkm', core_gathered, first_factor, precision=prec...  25.8 us
    all_to_all x1, blocking collectives, per_device(): lax.all_to_all(projected, 'col', split_axis=2, concat_axis=1, tiled=True)  20.6 us
    dot_general x1, matrix products, per_device(): jnp.einsum('cpqktz,yt->cpqkyz', weight_first, second_factor, precision=pr...  17.9 us
    dot_general x1, matrix products, per_device(): jnp.einsum('brkm,rqkm->bqkm', rank_spectrum[1], mode_weight[1], precision...  14.6 us
    dot_general x1, matrix products, per_device(): jnp.einsum('brkm,rqkm->bqkm', rank_spectrum[0], mode_weight[1], precision...  14.4 us
    dot_general x1, matrix products, per_device(): jnp.einsum('brkm,rqkm->bqkm', rank_spectrum[0], mode_weight[0], precision...  14.4 us
  transfers between devices with their start and end apart: 2, of which 2 were waited for; matrix products, arithmetic and copies ran while one was open for 3% of the time, Pallas kernels for 0%

commit v1 on v0

--- a/solution.py
+++ b/solution.py
@@ -2,6 +2,7 @@
 import jax.numpy as jnp
 from jax import lax
 from jax.sharding import PartitionSpec as P
+from jax.lax import all_to_all, axis_size
 
 precise = lax.Precision.HIGHEST
 
@@ -26,7 +27,16 @@
     mode_weight = jnp.einsum("cpqktz,yt->cpqkyz", weight_first, second_factor, precision=precise)
     mode_weight = mode_weight.reshape(2, rank_local, rank_out, rows_first, -1)
     projected = jnp.einsum("cbikm,ir->cbrkm", spectrum, input_factor, precision=precise)
-    rank_spectrum = lax.all_to_all(projected, "col", split_axis=2, concat_axis=1, tiled=True)
+    tables_solve = lambda content, join_dim, dim_no: jnp.concatenate(
+        all_to_all(
+            jnp.stack(jnp.split(content, axis_size("col"), axis=join_dim)),
+            "col",
+            split_axis=0,
+            concat_axis=0,
+        ),
+        axis=dim_no,
+    )
+    rank_spectrum = tables_solve(projected, 2, 1)
     real_part = jnp.einsum(
         "brkm,rqkm->bqkm", rank_spectrum[0], mode_weight[0], precision=precise
     ) - jnp.einsum("brkm,rqkm->bqkm", rank_spectrum[1], mode_weight[1], precision=precise)

time: 383 us -> 381 us (level)
  transfers between devices with their start and end apart: 2 -> 2, of which waited for: 2 -> 2; matrix products, arithmetic and copies ran while one was open for 3% -> 2% of each run, Pallas kernels for 0% -> 0%
where the time goes in v1:
time: 381 us; the launch traced here: 377 us
  waiting for transfers between devices  181 us (48%)
  matrix products  114 us (30%)
  local copies, waits for them, and re-layouts  40.7 us (11%)
  blocking collectives  20.8 us (5%)
  between operations  13.9 us (4%)
  other arithmetic  6.1 us (2%)
    all_gather x1, waiting for transfers between devices, per_device(): core_gathered = lax.all_gather(core_third, ('mx', 'my'), axis=3, tiled=True)  91.2 us
    reduce_scatter x1, waiting for transfers between devices, per_device(): lax.psum_scatter(mode_values, 'col', scatter_dimension=1, tiled=True)  89.9 us
    dot_general x1, matrix products, per_device(): jnp.einsum('cpqsm,ks->cpqkm', core_gathered, first_factor, precision=prec...  25.7 us
    all_to_all x1, blocking collectives, per_device(): all_to_all(jnp.stack(jnp.split(content, axis_size('col'), axis=join_dim))...  20.8 us
    dot_general x1, matrix products, per_device(): jnp.einsum('cpqktz,yt->cpqkyz', weight_first, second_factor, precision=pr...  17.7 us
    dot_general x1, matrix products, per_device(): jnp.einsum('brkm,rqkm->bqkm', rank_spectrum[1], mode_weight[1], precision...  14.6 us
    dot_general x1, matrix products, per_device(): jnp.einsum('brkm,rqkm->bqkm', rank_spectrum[0], mode_weight[1], precision...  14.4 us
    dot_general x1, matrix products, per_device(): jnp.einsum('brkm,rqkm->bqkm', rank_spectrum[0], mode_weight[0], precision...  14.4 us
  transfers between devices with their start and end apart: 2, of which 2 were waited for; matrix products, arithmetic and copies ran while one was open for 2% of the time, Pallas kernels for 0%

profile of v1, /device:TPU:1, one launch (start us, length us, event | category | flops | bytes accessed | tf_op | source)
XLA Modules:
  0.0 376.8 jit_solution(9017947949962841470)
XLA Ops:
  6.5 0.0 copy-start
  6.5 0.0 copy-start.4
  6.5 0.0 all-gather.2.cloned.1.call-start
  6.5 1.6 copy-done
  8.1 3.9 %fusion.22 = f32[2,8,64,16,16]{2,4,3,1,0:T(8,128)} fusion(f32[2,8,64,1,16,16]{2,5,4,3,1,0:T(8,128)S(1)} %copy-done, f32[16,16]{1,0:T(8,128)} %param.13), kind=kOutput, calls=%fused_computation.17 | convolution fusion | flops 50331648 | bytes 2098176 | tf_op jit(solution)/shard_map/cpqstu,zu->cpqstz/dot_general | solution.py:18
  12.1 3.2 copy.33
  15.2 0.0 all-gather.2.cloned.1.call-update
  15.2 0.0 reduce-scatter.2.cloned.1.call-start
  15.3 0.0 copy-done.4
  15.3 3.1 fusion.26
  18.6 20.8 %all_to_all.5 = f32[8,2,2,8,8,128]{5,3,4,2,1,0:T(8,128)S(1)} all-to-all(f32[8,2,2,8,8,128]{5,3,4,2,1,0:T(8,128)S(1)} %fusion.30), channel_id=1, replica_groups=mesh['mx'=4,'my'=4,'col'=8] {'col'}, dimensions={0} | all-to-all | bytes 2097152 | tf_op jit(solution)/shard_map/all_to_all | solution.py:31
  39.4 0.1 fusion.44
  39.6 0.0 copy-start.6
  39.6 2.6 copy.40
  42.2 2.6 copy.43
  44.8 91.2 %all-gather.2.cloned.1.call-done = f32[2,8,64,16,256]{4,2,1,0,3:T(8,128)} async-done(((f32[2,8,64,1,256]{4,2,1,0,3:T(8,128)}), f32[2,8,64,16,256]{4,2,1,0,3:T(8,128)}) %all-gather.2.cloned.1.call-update) | async-done | bytes 16777232 | tf_op jit(solution)/shard_map/all_gather | solution.py:22
  136.1 0.0 copy-done.6
  136.1 25.7 %fusion.16 = f32[2,8,64,8,256]{4,3,2,1,0:T(8,128)} fusion(f32[2,8,64,16,256]{4,2,1,0,3:T(8,128)} %all-gather.2.cloned.1.call-done, f32[8,16]{1,0:T(8,128)S(1)} %copy-done.6), kind=kOutput, calls=%fused_computation.15 | convolution fusion | flops 402653184 | bytes 25166336 | tf_op jit(solution)/shard_map/cpqsm,ks->cpqkm/dot_general | solution.py:23
  161.8 0.0 copy-start.7
  161.8 12.4 %copy.35 = f32[2,8,64,8,256]{2,4,3,1,0:T(8,128)} copy(f32[2,8,64,8,256]{4,3,2,1,0:T(8,128)} %fusion.16) | data formatting | bytes 16777216 | tf_op jit(solution)/shard_map/cpqsm,ks->cpqkm/transpose | solution.py:23
  174.2 0.0 copy-done.7
  174.2 17.7 %fusion.19 = f32[2,8,64,8,8,16]{2,4,5,3,1,0:T(8,128)S(1)} fusion(f32[2,8,64,8,16,16]{2,5,4,3,1,0:T(8,128)} %bitcast.89, f32[8,16]{1,0:T(8,128)S(1)} %copy-done.7), kind=kOutput, calls=%fused_computation.16 | convolution fusion | flops 201326592 | bytes 12583424 | tf_op jit(solution)/shard_map/cpqktz,yt->cpqkyz/dot_general | solution.py:27
  191.9 1.1 fusion.43
  192.9 0.9 copy.37
  193.9 0.0 copy-start.2
  193.9 0.9 copy.41
  194.8 1.2 copy-done.2
  196.0 0.0 copy-start.3
  196.0 14.4 %fusion.4 = f32[8,128,64,16]{2,3,1,0:T(8,128)S(1)} fusion(f32[16,8,8,128]{0,1,3,2:T(8,128)S(1)} %copy-done.2, f32[8,64,8,128]{1,3,2,0:T(8,128)S(1)} %bitcast.90), kind=kOutput, calls=%fused_computation.7 | convolution fusion | flops 100663296 | bytes 6815744 | tf_op jit(solution)/shard_map/brkm,rqkm->bqkm/dot_general | solution.py:43
  210.4 0.0 copy-done.3
  210.4 14.6 %fusion.6 = f32[8,128,64,16]{2,3,1,0:T(8,128)S(1)} fusion(f32[16,8,8,128]{0,1,3,2:T(8,128)S(1)} %copy-done.3, f32[8,64,8,128]{1,3,2,0:T(8,128)S(1)} %bitcast.91), kind=kOutput, calls=%fused_computation.9 | convolution fusion | flops 100663296 | bytes 6815744 | tf_op jit(solution)/shard_map/brkm,rqkm->bqkm/dot_general | solution.py:42
  225.1 14.3 %add_bitcast_fusion = f32[1,16,64,8,128]{2,1,4,3,0:T(8,128)S(1)} fusion(f32[8,128,64,16]{2,3,1,0:T(8,128)S(1)} %fusion.4, f32[16,8,8,128]{0,1,3,2:T(8,128)S(1)} %copy-done.3, f32[8,64,8,128]{1,3,2,0:T(8,128)S(1)} %bitcast.87), kind=kOutput, calls=%fused_computation.5 | convolution fusion | flops 101711872 | bytes 11010048 | tf_op jit(solution)/shard_map/brkm,rqkm->bqkm/dot_general | solution.py:45
  239.4 14.4 %subtract_bitcast_fusion = f32[1,16,64,8,128]{2,1,4,3,0:T(8,128)S(1)} fusion(f32[8,128,64,16]{2,3,1,0:T(8,128)S(1)} %fusion.6, f32[16,8,8,128]{0,1,3,2:T(8,128)S(1)} %copy-done.2, f32[8,64,8,128]{1,3,2,0:T(8,128)S(1)} %bitcast.88), kind=kOutput, calls=%fused_computation.6 | convolution fusion | flops 101711872 | bytes 11010048 | tf_op jit(solution)/shard_map/brkm,rqkm->bqkm/dot_general | solution.py:40
  253.8 6.1 %pad_maximum_fusion = f32[2,16,64,8,128]{2,1,4,3,0:T(8,128)} fusion(f32[1,16,64,8,128]{2,1,4,3,0:T(8,128)S(1)} %add_bitcast_fusion, f32[1,16,64,8,128]{2,1,4,3,0:T(8,128)S(1)} %subtract_bitcast_fusion), kind=kLoop, calls=%fused_computation | loop fusion | flops 2097152 | bytes 16777216 | tf_op jit(solution)/shard_map/stack | solution.py:46
  259.9 11.0 %copy.48 = f32[2,16,64,8,128]{4,3,2,0,1:T(8,128)} copy(f32[2,16,64,8,128]{2,1,4,3,0:T(8,128)} %pad_maximum_fusion) | data formatting | bytes 16777216 | tf_op jit(solution)/shard_map/stack | solution.py:46
  270.9 0.0 copy-start.5
  270.9 0.0 reduce-scatter.2.cloned.1.call-update
  270.9 0.0 copy-start.1
  270.9 89.9 %reduce-scatter.2.cloned.1.call-done = f32[2,2,64,8,128]{4,3,2,0,1:T(8,128)} async-done(((f32[2,16,64,8,128]{4,3,2,0,1:T(8,128)}), f32[2,2,64,8,128]{4,3,2,0,1:T(8,128)}) %reduce-scatter.2.cloned.1.call-update) | async-done | bytes 1048592 | tf_op jit(solution)/shard_map/reduce_scatter | solution.py:47
  360.8 0.0 copy-done.5
  360.8 6.0 %convolution_bitcast_fusion = f32[2,2,128,8,128]{2,4,3,1,0:T(8,128)} fusion(f32[2,2,64,8,128]{4,3,2,0,1:T(8,128)} %reduce-scatter.2.cloned.1.call-done, f32[128,64]{0,1:T(8,128)S(1)} %copy-done.5), kind=kOutput, calls=%fused_computation.21 | convolution fusion | flops 402653184 | bytes 3178496 | tf_op jit(solution)/shard_map/oq,cbqkm->cbokm/dot_general | solution.py:48
  366.8 2.9 copy.50
  369.7 0.0 copy-done.1
  (8 shorter events, 0.2 us)
Async XLA Ops:
  6.5 1.6 copy-start
  6.5 8.8 %copy-start.4 = (f32[128,64]{0,1:T(8,128)S(1)}, f32[128,64]{0,1:T(8,128)}, u32[]{:S(2)}) copy-start(f32[128,64]{0,1:T(8,128)} %param.9) | copy-start | bytes 98308
  6.5 129.5 %all-gather.2.cloned.1.call-start = ((), (), s32[]{:S(2)}) async-start(), calls=%async_computation.2 | async-start | bytes 17825792 | tf_op jit(solution)/shard_map/all_gather | solution.py:22
  15.2 345.6 %reduce-scatter.2.cloned.1.call-start = ((), (), s32[]{:S(2)}) async-start(), calls=%async_computation.3 | async-start | bytes 9437184 | tf_op jit(solution)/shard_map/reduce_scatter | solution.py:47
  39.6 96.5 %copy-start.6 = (f32[8,16]{1,0:T(8,128)S(1)}, f32[8,16]{1,0:T(8,128)}, u32[]{:S(2)}) copy-start(f32[8,16]{1,0:T(8,128)} %param.11) | copy-start | bytes 1540
  161.8 12.4 %copy-start.7 = (f32[8,16]{1,0:T(8,128)S(1)}, f32[8,16]{1,0:T(8,128)}, u32[]{:S(2)}) copy-start(f32[8,16]{1,0:T(8,128)} %param.12) | copy-start | bytes 1540
  193.9 2.2 copy-start.2
  196.0 14.4 %copy-start.3 = (f32[16,8,8,128]{0,1,3,2:T(8,128)S(1)}, f32[16,8,8,128]{0,1,3,2:T(8,128)}, u32[]{:S(2)}) copy-start(f32[16,8,8,128]{0,1,3,2:T(8,128)} %copy.43) | copy-start | bytes 1572868
  270.9 89.9 %copy-start.5 = (f32[128,64]{0,1:T(8,128)S(1)}, f32[128,64]{0,1:T(8,128)}, u32[]{:S(2)}) copy-start(f32[128,64]{0,1:T(8,128)} %param.10) | copy-start | bytes 98308
  270.9 98.8 %copy-start.1 = (f32[2,8,64,1,16,16]{2,5,4,3,1,0:T(8,128)S(1)}, f32[2,8,64,1,16,16]{2,5,4,3,1,0:T(8,128)}, u32[]{:S(2)}) copy-start(f32[2,8,64,1,16,16]{2,5,4,3,1,0:T(8,128)} %param.8) | copy-start | bytes 3145732
Sparse Core Ops, SparseCore 0:
  15.4 120.6 all-gather.1
  271.0 89.7 reduce-scatter.1
